TPU v7x, 32 devices: a whole 2x2x4 slice. The times are simulated.
32 devices in a mesh: row: 4 (over z), col: 2 (over x), depth: 4 (over y, core).
Axes of the slice: x: 2, y: 2, z: 4, core: 2. Of those that a mesh axis runs over, the one named last changes fastest.
Arguments:
- pair_input: bfloat16 [192, 192, 128], P('row', ('col', 'depth')), may hold values from -40 to 40
- in_gain: float32 [128], replicated, may hold values from 0.1 to 1.9
- in_shift: float32 [128], replicated, may hold values from -3 to 3
- w_proj: bfloat16 [128, 512], replicated, may hold values from -0.5 to 0.5
- w_gate: bfloat16 [128, 128], replicated, may hold values from -0.5 to 0.5
- out_gain: float32 [128], replicated, may hold values from 0.1 to 1.9
- out_shift: float32 [128], replicated, may hold values from -3 to 3
- w_out: bfloat16 [128, 128], replicated, may hold values from -0.5 to 0.5
Outputs:
- update: bfloat16 [192, 192, 128], P('row', ('col', 'depth'))
All inputs are finite; a program needn't handle non-finite values.
Results may differ from a plain program's by a relative error of at most 0.013.
Values may be sent and summed in bfloat16 or wider, within the bound.
A program may use at most 64 MiB of HBM per device.

v0:
```python
import jax
import jax.numpy as jnp
from jax import lax
from jax.sharding import PartitionSpec as P


def layer_norm(values, scaling, offsets):
    average = jnp.mean(values, axis=-1, keepdims=True)
    centred = values - average
    variance = jnp.mean(centred * centred, axis=-1, keepdims=True)
    return centred * lax.rsqrt(variance + 1e-05) * scaling + offsets


def gated_sides(normed, w_proj):
    channels = w_proj.shape[1] // 4
    projected = jnp.einsum("xyc,cd->xyd", normed, w_proj, preferred_element_type=jnp.float32)
    left_side = (
        jax.nn.sigmoid(projected[..., :channels]) * projected[..., channels : 2 * channels]
    ).astype(jnp.bfloat16)
    right_side = (
        jax.nn.sigmoid(projected[..., 2 * channels : 3 * channels]) * projected[..., 3 * channels :]
    ).astype(jnp.bfloat16)
    return (left_side, right_side)


def reorder_channels(values, row_count, other_count):
    shape_rest = values.shape[1:]
    grouped = values.reshape((row_count, other_count, -1) + shape_rest)
    return jnp.swapaxes(grouped, 0, 1).reshape(values.shape)


def per_device(pair_input, in_gain, in_shift, w_proj, w_gate, out_gain, out_shift, w_out):
    row_count = lax.axis_size("row")
    col_count = lax.axis_size("col")
    depth_count = lax.axis_size("depth")
    normed = layer_norm(pair_input.astype(jnp.float32), in_gain, in_shift).astype(jnp.bfloat16)
    left_side, right_side = gated_sides(normed, w_proj)
    left_all, right_all = (
        lax.all_to_all(
            lax.all_to_all(left_side, "row", split_axis=2, concat_axis=0, tiled=True),
            ("col", "depth"),
            split_axis=2,
            concat_axis=1,
            tiled=True,
        ),
        lax.all_to_all(
            lax.all_to_all(right_side, "row", split_axis=2, concat_axis=0, tiled=True),
            ("col", "depth"),
            split_axis=2,
            concat_axis=1,
            tiled=True,
        ),
    )
    planes = jnp.einsum("kic,kjc->ijc", left_all, right_all, preferred_element_type=jnp.float32)
    product = lax.all_to_all(
        lax.all_to_all(planes.astype(jnp.bfloat16), "row", split_axis=0, concat_axis=2, tiled=True),
        ("col", "depth"),
        split_axis=1,
        concat_axis=2,
        tiled=True,
    ).astype(planes.dtype)
    other_count = col_count * depth_count
    used_gain = reorder_channels(out_gain, row_count, other_count)
    used_shift = reorder_channels(out_shift, row_count, other_count)
    used_out = reorder_channels(w_out, row_count, other_count)
    product_norm = layer_norm(product, used_gain, used_shift).astype(jnp.bfloat16)
    gating = jax.nn.sigmoid(
        jnp.einsum("xyc,cd->xyd", normed, w_gate, preferred_element_type=jnp.float32)
    )
    projected_out = jnp.einsum(
        "xyc,cd->xyd", product_norm, used_out, preferred_element_type=jnp.float32
    )
    return (gating * projected_out).astype(jnp.bfloat16)


def solution(mesh):
    placed = (P("row", ("col", "depth"), None), P(), P(), P(), P(), P(), P(), P())
    return jax.shard_map(
        per_device,
        mesh=mesh,
        in_specs=placed,
        out_specs=P("row", ("col", "depth"), None),
        check_vma=False,
    )
```

profile of v0, /device:TPU:0, one launch (start us, length us, event | category | flops | bytes accessed | tf_op | source)
XLA Modules:
  0.0 87.3 jit_solution(1574282504677348500)
XLA Ops:
  0.0 1.2 %convert_reduce_fusion = f32[48,24]{1,0:T(8,128)S(1)} fusion(bf16[48,24,128]{2,1,0:T(8,128)(2,1)} %param.8), kind=kLoop, calls=%fused_computation.18 | loop fusion | flops 293760 | bytes 299520 | tf_op jit(solution)/shard_map/reduce_sum | solution.py:8
  1.4 1.4 %fusion.15 = f32[48,24]{1,0:T(8,128)S(1)} fusion(bf16[48,24,128]{2,1,0:T(8,128)(2,1)} %param.8, f32[48,24]{1,0:T(8,128)S(1)} %copy.86), kind=kLoop, calls=%fused_computation.21 | loop fusion | flops 588672 | bytes 304128 | tf_op jit(solution)/shard_map/reduce_sum | solution.py:10
  2.9 1.6 %fusion.27 = f32[48,24,512]{2,1,0:T(8,128)S(1)} fusion(bf16[128,512]{1,0:T(8,128)(2,1)S(1)} %copy-done, bf16[48,24,128]{2,1,0:T(8,128)(2,1)} %param.8, f32[128]{0:T(128)} %param.10, f32[128]{0:T(128)} %param.9, f32[48,24]{1,0:T(8,128)S(1)} %copy.88, f32[48,24]{1,0:T(8,128)S(1)} %copy.86), kind=kOutput, calls=%fused_computation.37 | convolution fusion | flops 151879680 | bytes 2795520 | tf_op jit(solution)/shard_map/xyc,cd->xyd/dot_general | solution.py:16
  4.5 0.3 fusion.19
  4.8 0.5 copy.94
  5.3 2.0 %reshape.59 = bf16[4,2,18432]{2,1,0:T(2,128)(2,1)} reshape(bf16[128,24,48]{2,1,0:T(8,128)(2,1)S(1)} %bitcast.78) | data formatting | bytes 589824
  7.3 6.3 %all-to-all-start.2 = ((bf16[4,2,18432]{2,1,0:T(2,128)(2,1)}), bf16[4,2,18432]{2,1,0:T(2,128)(2,1)S(1)}, u32[]{:S(2)}, u32[]{:S(2)}) async-start(bf16[4,2,18432]{2,1,0:T(2,128)(2,1)} %reshape.59), calls=%async_computation.2 | async-start | bytes 589824 | tf_op jit(solution)/shard_map/all_to_all | solution.py:40
  13.7 0.5 copy.89
  14.1 2.0 %reshape.57 = bf16[4,2,18432]{2,1,0:T(2,128)(2,1)} reshape(bf16[128,24,48]{2,1,0:T(8,128)(2,1)S(1)} %bitcast.79) | data formatting | bytes 589824
  16.2 7.1 %all-to-all-done.2 = bf16[4,2,18432]{2,1,0:T(2,128)(2,1)S(1)} async-done(((bf16[4,2,18432]{2,1,0:T(2,128)(2,1)}), bf16[4,2,18432]{2,1,0:T(2,128)(2,1)S(1)}, u32[]{:S(2)}, u32[]{:S(2)}) %all-to-all-start.2) | async-done | bytes 294944 | tf_op jit(solution)/shard_map/all_to_all | solution.py:40
  23.3 3.5 %all-to-all-start = ((bf16[4,2,18432]{2,1,0:T(2,128)(2,1)}), bf16[4,2,18432]{2,1,0:T(2,128)(2,1)S(1)}, u32[]{:S(2)}, u32[]{:S(2)}) async-start(bf16[4,2,18432]{2,1,0:T(2,128)(2,1)} %reshape.57), calls=%async_computation | async-start | bytes 589824 | tf_op jit(solution)/shard_map/all_to_all | solution.py:47
  26.7 0.8 reshape.60
  27.5 0.6 copy.115
  28.1 1.2 %reshape.56 = bf16[192,24,32]{0,1,2:T(8,128)(2,1)} reshape(bf16[4,48,24,32]{1,0,2,3:T(4,128)(2,1)S(1)} %copy.115) | data formatting | bytes 589824 | tf_op jit(solution)/shard_map/all_to_all | solution.py:40
  29.3 5.5 %all-to-all-done = bf16[4,2,18432]{2,1,0:T(2,128)(2,1)S(1)} async-done(((bf16[4,2,18432]{2,1,0:T(2,128)(2,1)}), bf16[4,2,18432]{2,1,0:T(2,128)(2,1)S(1)}, u32[]{:S(2)}, u32[]{:S(2)}) %all-to-all-start) | async-done | bytes 294944 | tf_op jit(solution)/shard_map/all_to_all | solution.py:47
  34.9 3.7 %all-to-all-start.3 = ((bf16[192,24,32]{0,1,2:T(8,128)(2,1)}), bf16[192,24,32]{0,1,2:T(8,128)(2,1)S(1)}, u32[]{:S(2)}, u32[]{:S(2)}) async-start(bf16[192,24,32]{0,1,2:T(8,128)(2,1)} %reshape.56), calls=%async_computation.3 | async-start | bytes 786432 | tf_op jit(solution)/shard_map/all_to_all | solution.py:39
  38.6 0.8 reshape.58
  39.4 0.6 copy.113
  40.0 1.2 %reshape.55 = bf16[192,24,32]{0,1,2:T(8,128)(2,1)} reshape(bf16[4,48,24,32]{1,0,2,3:T(4,128)(2,1)S(1)} %copy.113) | data formatting | bytes 589824 | tf_op jit(solution)/shard_map/all_to_all | solution.py:47
  41.2 4.9 %all-to-all-done.3 = bf16[192,24,32]{0,1,2:T(8,128)(2,1)S(1)} async-done(((bf16[192,24,32]{0,1,2:T(8,128)(2,1)}), bf16[192,24,32]{0,1,2:T(8,128)(2,1)S(1)}, u32[]{:S(2)}, u32[]{:S(2)}) %all-to-all-start.3) | async-done | bytes 294944 | tf_op jit(solution)/shard_map/all_to_all | solution.py:39
  46.0 3.5 %all-to-all-start.1 = ((bf16[192,24,32]{0,1,2:T(8,128)(2,1)}), bf16[192,24,32]{0,1,2:T(8,128)(2,1)S(1)}, u32[]{:S(2)}, u32[]{:S(2)}) async-start(bf16[192,24,32]{0,1,2:T(8,128)(2,1)} %reshape.55), calls=%async_computation.1 | async-start | bytes 786432 | tf_op jit(solution)/shard_map/all_to_all | solution.py:46
  49.5 7.3 %all-to-all-done.1 = bf16[192,24,32]{0,1,2:T(8,128)(2,1)S(1)} async-done(((bf16[192,24,32]{0,1,2:T(8,128)(2,1)}), bf16[192,24,32]{0,1,2:T(8,128)(2,1)S(1)}, u32[]{:S(2)}, u32[]{:S(2)}) %all-to-all-start.1) | async-done | bytes 294944 | tf_op jit(solution)/shard_map/all_to_all | solution.py:46
  57.5 14.1 %all_to_all.99 = bf16[192,192,4]{1,2,0:T(4,128)(2,1)S(1)} all-to-all(bf16[192,192,4]{1,2,0:T(4,128)(2,1)S(1)} %copy.100), channel_id=1, replica_groups=mesh['row'=4,'col'=2,'depth'=4] {'row'}, dimensions={0} | all-to-all | bytes 589824 | tf_op jit(solution)/shard_map/all_to_all | solution.py:56
  71.8 0.7 copy.103
  72.4 1.9 %reshape.61 = bf16[8,2,9216]{2,1,0:T(2,128)(2,1)} reshape(bf16[192,16,48]{2,1,0:T(8,128)(2,1)S(1)} %bitcast.76) | data formatting | bytes 589824
  74.3 3.6 %all-to-all-start.5 = ((bf16[8,2,9216]{2,1,0:T(2,128)(2,1)}), bf16[8,2,9216]{2,1,0:T(2,128)(2,1)S(1)}, u32[]{:S(2)}, u32[]{:S(2)}) async-start(bf16[8,2,9216]{2,1,0:T(2,128)(2,1)} %reshape.61), calls=%async_computation.5 | async-start | bytes 589824 | tf_op jit(solution)/shard_map/all_to_all | solution.py:55
  78.6 0.5 fusion.10
  79.1 4.9 %all-to-all-done.5 = bf16[8,2,9216]{2,1,0:T(2,128)(2,1)S(1)} async-done(((bf16[8,2,9216]{2,1,0:T(2,128)(2,1)}), bf16[8,2,9216]{2,1,0:T(2,128)(2,1)S(1)}, u32[]{:S(2)}, u32[]{:S(2)}) %all-to-all-start.5) | async-done | bytes 294944 | tf_op jit(solution)/shard_map/all_to_all | solution.py:55
  84.1 0.8 reshape.62
  85.3 0.4 fusion.7
  86.0 0.3 copy.110
  86.3 1.0 %fusion.11 = bf16[48,24,128]{2,1,0:T(8,128)(2,1)} fusion(f32[48,24,128]{2,1,0:T(8,128)S(1)} %fusion.10, bf16[48,24,128]{2,1,0:T(8,128)(2,1)S(1)} %copy.110, bf16[128,128,1]{1,0,2:T(8,128)(2,1)S(1)} %bitcast.86), kind=kOutput, calls=%fused_computation.15 | convolution fusion | flops 38043648 | bytes 1212416 | tf_op jit(solution)/shard_map/xyc,cd->xyd/dot_general | solution.py:70
  (40 shorter events, 2.3 us)
Async XLA Ops:
  0.0 2.9 %copy-start = (bf16[128,512]{1,0:T(8,128)(2,1)S(1)}, bf16[128,512]{1,0:T(8,128)(2,1)}, u32[]{:S(2)}) copy-start(bf16[128,512]{1,0:T(8,128)(2,1)} %param.11) | copy-start | bytes 393220
  7.3 16.0 %all-to-all-start.2 = ((bf16[4,2,18432]{2,1,0:T(2,128)(2,1)}), bf16[4,2,18432]{2,1,0:T(2,128)(2,1)S(1)}, u32[]{:S(2)}, u32[]{:S(2)}) async-start(bf16[4,2,18432]{2,1,0:T(2,128)(2,1)} %reshape.59), calls=%async_computation.2 | async-start | bytes 589824 | tf_op jit(solution)/shard_map/all_to_all | solution.py:40
  23.3 11.6 %all-to-all-start = ((bf16[4,2,18432]{2,1,0:T(2,128)(2,1)}), bf16[4,2,18432]{2,1,0:T(2,128)(2,1)S(1)}, u32[]{:S(2)}, u32[]{:S(2)}) async-start(bf16[4,2,18432]{2,1,0:T(2,128)(2,1)} %reshape.57), calls=%async_computation | async-start | bytes 589824 | tf_op jit(solution)/shard_map/all_to_all | solution.py:47
  34.9 11.2 %all-to-all-start.3 = ((bf16[192,24,32]{0,1,2:T(8,128)(2,1)}), bf16[192,24,32]{0,1,2:T(8,128)(2,1)S(1)}, u32[]{:S(2)}, u32[]{:S(2)}) async-start(bf16[192,24,32]{0,1,2:T(8,128)(2,1)} %reshape.56), calls=%async_computation.3 | async-start | bytes 786432 | tf_op jit(solution)/shard_map/all_to_all | solution.py:39
  46.0 10.8 %all-to-all-start.1 = ((bf16[192,24,32]{0,1,2:T(8,128)(2,1)}), bf16[192,24,32]{0,1,2:T(8,128)(2,1)S(1)}, u32[]{:S(2)}, u32[]{:S(2)}) async-start(bf16[192,24,32]{0,1,2:T(8,128)(2,1)} %reshape.55), calls=%async_computation.1 | async-start | bytes 786432 | tf_op jit(solution)/shard_map/all_to_all | solution.py:46
  71.7 6.3 %copy-start.5 = (f32[128]{0:T(128)S(1)}, f32[128]{0:T(128)}, u32[]{:S(2)}) copy-start(f32[128]{0:T(128)} %param.13) | copy-start | bytes 1540
  71.7 6.5 %copy-start.6 = (f32[128]{0:T(128)S(1)}, f32[128]{0:T(128)}, u32[]{:S(2)}) copy-start(f32[128]{0:T(128)} %param.14) | copy-start | bytes 1540
  71.7 6.8 %copy-start.2 = (bf16[128,128]{1,0:T(8,128)(2,1)S(1)}, bf16[128,128]{1,0:T(8,128)(2,1)}, u32[]{:S(2)}) copy-start(bf16[128,128]{1,0:T(8,128)(2,1)} %param.15) | copy-start | bytes 98308
  71.7 6.8 %copy-start.1 = (bf16[48,24,128]{2,1,0:T(8,128)(2,1)S(1)}, bf16[48,24,128]{2,1,0:T(8,128)(2,1)}, u32[]{:S(2)}) copy-start(bf16[48,24,128]{2,1,0:T(8,128)(2,1)} %param.8) | copy-start | bytes 884740
  71.7 6.8 %copy-start.3 = (f32[128]{0:T(128)S(1)}, f32[128]{0:T(128)}, u32[]{:S(2)}) copy-start(f32[128]{0:T(128)} %param.10) | copy-start | bytes 1540
  71.7 6.8 %copy-start.4 = (f32[128]{0:T(128)S(1)}, f32[128]{0:T(128)}, u32[]{:S(2)}) copy-start(f32[128]{0:T(128)} %param.9) | copy-start | bytes 1540
  71.7 6.8 %copy-start.7 = (bf16[128,128]{1,0:T(8,128)(2,1)S(1)}, bf16[128,128]{1,0:T(8,128)(2,1)}, u32[]{:S(2)}) copy-start(bf16[128,128]{1,0:T(8,128)(2,1)} %param.12) | copy-start | bytes 98308
  74.3 9.7 %all-to-all-start.5 = ((bf16[8,2,9216]{2,1,0:T(2,128)(2,1)}), bf16[8,2,9216]{2,1,0:T(2,128)(2,1)S(1)}, u32[]{:S(2)}, u32[]{:S(2)}) async-start(bf16[8,2,9216]{2,1,0:T(2,128)(2,1)} %reshape.61), calls=%async_computation.5 | async-start | bytes 589824 | tf_op jit(solution)/shard_map/all_to_all | solution.py:55
where the time goes:
time: 88 us; the launch traced here: 87.3 us
  waiting for transfers between devices  29.8 us (34%)
  starting transfers between devices  20.6 us (23%)
  local copies, waits for them, and re-layouts  15.3 us (17%)
  blocking collectives  14.1 us (16%)
  other arithmetic  3.81 us (4%)
  matrix products  3.41 us (4%)
    all_to_all x1, blocking collectives, per_device(): lax.all_to_all(planes.astype(jnp.bfloat16), 'row', split_axis=0, concat_a...  14.1 us
    unnamed x22, local copies, waits for them, and re-layouts  8.3 us
    all_to_all x1, waiting for transfers between devices, per_device(): lax.all_to_all(lax.all_to_all(right_side, 'row', split_axis=2, concat_axi...  7.34 us
    all_to_all x1, waiting for transfers between devices, per_device(): lax.all_to_all(left_side, 'row', split_axis=2, concat_axis=0, tiled=True)  7.1 us
    all_to_all x1, starting transfers between devices, per_device(): lax.all_to_all(left_side, 'row', split_axis=2, concat_axis=0, tiled=True)  6.35 us
    all_to_all x1, waiting for transfers between devices, per_device(): lax.all_to_all(right_side, 'row', split_axis=2, concat_axis=0, tiled=True)  5.54 us
    all_to_all x1, waiting for transfers between devices, per_device(): lax.all_to_all(lax.all_to_all(planes.astype(jnp.bfloat16), 'row', split_a...  4.94 us
    all_to_all x1, waiting for transfers between devices, per_device(): lax.all_to_all(lax.all_to_all(left_side, 'row', split_axis=2, concat_axis...  4.88 us
  transfers between devices with their start and end apart: 5, of which 5 were waited for; matrix products, arithmetic and copies ran while one was open for 10% of the time, Pallas kernels for 0%

commit v1 on v0

--- a/solution.py
+++ b/solution.py
@@ -2,6 +2,12 @@
 import jax.numpy as jnp
 from jax import lax
 from jax.sharding import PartitionSpec as P
+
+
+def swap_blocks(x, axis, split, join):
+    pieces = jnp.split(x, lax.axis_size(axis), axis=split)
+    received = lax.all_to_all(jnp.stack(pieces), axis, 0, 0)
+    return jnp.concatenate(received, axis=join)
 
 
 def layer_norm(values, scaling, offsets):
@@ -44,7 +50,7 @@
             tiled=True,
         ),
         lax.all_to_all(
-            lax.all_to_all(right_side, "row", split_axis=2, concat_axis=0, tiled=True),
+            swap_blocks(right_side, "row", 2, 0),
             ("col", "depth"),
             split_axis=2,
             concat_axis=1,

time: 88 us -> 88.9 us (1.010)
    all_to_all x2, starting transfers between devices: 6.9 us -> 10.1 us  [the longest x1 6.35 us: swap_blocks(): received = lax.all_to_all(jnp.stack(pieces), axis, 0, 0)]
    all_to_all x1, starting transfers between devices: 6.35 us -> 3.45 us  [per_device(): lax.all_to_all(left_side, 'row', split_axis=2, concat_axis=0, tiled=True)]
    all_to_all x1, waiting for transfers between devices: 4.88 us -> 7.34 us  [per_device(): lax.all_to_all(lax.all_to_all(left_side, 'row', split_axis=2, concat_axis...]
    all_to_all x1, waiting for transfers between devices: 7.1 us -> 5.56 us  [per_device(): lax.all_to_all(left_side, 'row', split_axis=2, concat_axis=0, tiled=True)]
    all_to_all x3 -> x2, local copies, waits for them, and re-layouts: 1.81 us -> 0.64 us  [the longest x1 0.61 us: swap_blocks(): received = lax.all_to_all(jnp.stack(pieces), axis, 0, 0)]
    reshape x0 -> x1, local copies, waits for them, and re-layouts: none -> 1.17 us  [swap_blocks(): return jnp.concatenate(received, axis=join)]
    another operation x0 -> x2, local copies, waits for them, and re-layouts: none -> 1.08 us  [swap_blocks(): received = lax.all_to_all(jnp.stack(pieces), axis, 0, 0)]
    all_to_all x2, waiting for transfers between devices: 12.9 us -> 12 us  [the longest x1 7.1 us: swap_blocks(): received = lax.all_to_all(jnp.stack(pieces), axis, 0, 0)]
where the time goes in v1:
time: 88.9 us; the launch traced here: 88.2 us
  waiting for transfers between devices  30 us (34%)
  starting transfers between devices  20.4 us (23%)
  local copies, waits for them, and re-layouts  15.9 us (18%)
  blocking collectives  14.1 us (16%)
  other arithmetic  4.12 us (5%)
  matrix products  3.42 us (4%)
    all_to_all x1, blocking collectives, per_device(): lax.all_to_all(planes.astype(jnp.bfloat16), 'row', split_axis=0, concat_a...  14.1 us
    unnamed x22, local copies, waits for them, and re-layouts  8.3 us
    all_to_all x1, waiting for transfers between devices, per_device(): lax.all_to_all(lax.all_to_all(left_side, 'row', split_axis=2, concat_axis...  7.34 us
    all_to_all x1, waiting for transfers between devices, swap_blocks(): received = lax.all_to_all(jnp.stack(pieces), axis, 0, 0)  7.1 us
    all_to_all x1, starting transfers between devices, swap_blocks(): received = lax.all_to_all(jnp.stack(pieces), axis, 0, 0)  6.35 us
    all_to_all x1, waiting for transfers between devices, per_device(): lax.all_to_all(left_side, 'row', split_axis=2, concat_axis=0, tiled=True)  5.56 us
    all_to_all x1, waiting for transfers between devices, per_device(): lax.all_to_all(lax.all_to_all(planes.astype(jnp.bfloat16), 'row', split_a...  5.12 us
    all_to_all x1, waiting for transfers between devices, per_device(): lax.all_to_all(swap_blocks(right_side, 'row', 2, 0), ('col', 'depth'), sp...  4.87 us
  transfers between devices with their start and end apart: 5, of which 5 were waited for; matrix products, arithmetic and copies ran while one was open for 10% of the time, Pallas kernels for 0%

profile of v1, /device:TPU:0, one launch (start us, length us, event | category | flops | bytes accessed | tf_op | source)
XLA Modules:
  0.0 88.2 jit_solution(6928074093538055693)
XLA Ops:
  0.0 1.2 %convert_reduce_fusion = f32[48,24]{1,0:T(8,128)S(1)} fusion(bf16[48,24,128]{2,1,0:T(8,128)(2,1)} %param.8), kind=kLoop, calls=%fused_computation.19 | loop fusion | flops 293760 | bytes 299520 | tf_op jit(solution)/shard_map/reduce_sum | solution.py:14
  1.4 1.4 %fusion.15 = f32[48,24]{1,0:T(8,128)S(1)} fusion(bf16[48,24,128]{2,1,0:T(8,128)(2,1)} %param.8, f32[48,24]{1,0:T(8,128)S(1)} %copy.81), kind=kLoop, calls=%fused_computation.22 | loop fusion | flops 588672 | bytes 304128 | tf_op jit(solution)/shard_map/reduce_sum | solution.py:16
  2.9 1.6 %fusion.27 = f32[48,24,512]{2,1,0:T(8,128)S(1)} fusion(bf16[128,512]{1,0:T(8,128)(2,1)S(1)} %copy-done, bf16[48,24,128]{2,1,0:T(8,128)(2,1)} %param.8, f32[128]{0:T(128)} %param.10, f32[128]{0:T(128)} %param.9, f32[48,24]{1,0:T(8,128)S(1)} %copy.83, f32[48,24]{1,0:T(8,128)S(1)} %copy.81), kind=kOutput, calls=%fused_computation.42 | convolution fusion | flops 151879680 | bytes 2795520 | tf_op jit(solution)/shard_map/xyc,cd->xyd/dot_general | solution.py:22
  4.5 0.3 fusion.19
  5.1 0.3 pad_maximum_fusion
  5.4 0.8 copy.84
  6.2 2.0 %reshape.60 = bf16[4,2,18432]{2,1,0:T(2,128)(2,1)} reshape(bf16[4,24,32,48]{3,2,1,0:T(8,128)(2,1)S(1)} %bitcast.84) | data formatting | bytes 589824
  8.2 6.3 %all-to-all-start = ((bf16[4,2,18432]{2,1,0:T(2,128)(2,1)}), bf16[4,2,18432]{2,1,0:T(2,128)(2,1)S(1)}, u32[]{:S(2)}, u32[]{:S(2)}) async-start(bf16[4,2,18432]{2,1,0:T(2,128)(2,1)} %reshape.60), calls=%async_computation | async-start | bytes 589824 | tf_op jit(solution)/shard_map/all_to_all | solution.py:9
  14.6 0.5 copy.87
  15.1 2.0 %reshape.62 = bf16[4,2,18432]{2,1,0:T(2,128)(2,1)} reshape(bf16[128,24,48]{2,1,0:T(8,128)(2,1)S(1)} %bitcast.83) | data formatting | bytes 589824
  17.1 7.1 %all-to-all-done = bf16[4,2,18432]{2,1,0:T(2,128)(2,1)S(1)} async-done(((bf16[4,2,18432]{2,1,0:T(2,128)(2,1)}), bf16[4,2,18432]{2,1,0:T(2,128)(2,1)S(1)}, u32[]{:S(2)}, u32[]{:S(2)}) %all-to-all-start) | async-done | bytes 294944 | tf_op jit(solution)/shard_map/all_to_all | solution.py:9
  24.2 3.5 %all-to-all-start.2 = ((bf16[4,2,18432]{2,1,0:T(2,128)(2,1)}), bf16[4,2,18432]{2,1,0:T(2,128)(2,1)S(1)}, u32[]{:S(2)}, u32[]{:S(2)}) async-start(bf16[4,2,18432]{2,1,0:T(2,128)(2,1)} %reshape.62), calls=%async_computation.2 | async-start | bytes 589824 | tf_op jit(solution)/shard_map/all_to_all | solution.py:46
  27.7 0.8 reshape.61
  28.4 0.6 copy.85
  29.1 1.2 %reshape.50 = bf16[192,24,32]{0,1,2:T(8,128)(2,1)} reshape(bf16[4,48,24,32]{1,0,2,3:T(4,128)(2,1)S(1)} %copy.85) | data formatting | bytes 589824 | tf_op jit(solution)/shard_map/reshape | solution.py:10
  30.2 5.6 %all-to-all-done.2 = bf16[4,2,18432]{2,1,0:T(2,128)(2,1)S(1)} async-done(((bf16[4,2,18432]{2,1,0:T(2,128)(2,1)}), bf16[4,2,18432]{2,1,0:T(2,128)(2,1)S(1)}, u32[]{:S(2)}, u32[]{:S(2)}) %all-to-all-start.2) | async-done | bytes 294944 | tf_op jit(solution)/shard_map/all_to_all | solution.py:46
  35.8 3.7 %all-to-all-start.1 = ((bf16[192,24,32]{0,1,2:T(8,128)(2,1)}), bf16[192,24,32]{0,1,2:T(8,128)(2,1)S(1)}, u32[]{:S(2)}, u32[]{:S(2)}) async-start(bf16[192,24,32]{0,1,2:T(8,128)(2,1)} %reshape.50), calls=%async_computation.1 | async-start | bytes 786432 | tf_op jit(solution)/shard_map/all_to_all | solution.py:52
  39.5 0.8 reshape.63
  40.3 0.6 copy.106
  40.9 1.2 %reshape.59 = bf16[192,24,32]{0,1,2:T(8,128)(2,1)} reshape(bf16[4,48,24,32]{1,0,2,3:T(4,128)(2,1)S(1)} %copy.106) | data formatting | bytes 589824 | tf_op jit(solution)/shard_map/all_to_all | solution.py:46
  42.1 4.9 %all-to-all-done.1 = bf16[192,24,32]{0,1,2:T(8,128)(2,1)S(1)} async-done(((bf16[192,24,32]{0,1,2:T(8,128)(2,1)}), bf16[192,24,32]{0,1,2:T(8,128)(2,1)S(1)}, u32[]{:S(2)}, u32[]{:S(2)}) %all-to-all-start.1) | async-done | bytes 294944 | tf_op jit(solution)/shard_map/all_to_all | solution.py:52
  47.0 3.5 %all-to-all-start.3 = ((bf16[192,24,32]{0,1,2:T(8,128)(2,1)}), bf16[192,24,32]{0,1,2:T(8,128)(2,1)S(1)}, u32[]{:S(2)}, u32[]{:S(2)}) async-start(bf16[192,24,32]{0,1,2:T(8,128)(2,1)} %reshape.59), calls=%async_computation.3 | async-start | bytes 786432 | tf_op jit(solution)/shard_map/all_to_all | solution.py:45
  50.5 7.3 %all-to-all-done.3 = bf16[192,24,32]{0,1,2:T(8,128)(2,1)S(1)} async-done(((bf16[192,24,32]{0,1,2:T(8,128)(2,1)}), bf16[192,24,32]{0,1,2:T(8,128)(2,1)S(1)}, u32[]{:S(2)}, u32[]{:S(2)}) %all-to-all-start.3) | async-done | bytes 294944 | tf_op jit(solution)/shard_map/all_to_all | solution.py:45
  58.4 14.1 %all_to_all.86 = bf16[192,192,4]{1,2,0:T(4,128)(2,1)S(1)} all-to-all(bf16[192,192,4]{1,2,0:T(4,128)(2,1)S(1)} %copy.93), channel_id=1, replica_groups=mesh['row'=4,'col'=2,'depth'=4] {'row'}, dimensions={0} | all-to-all | bytes 589824 | tf_op jit(solution)/shard_map/all_to_all | solution.py:62
  72.7 0.7 copy.96
  73.4 1.9 %reshape.64 = bf16[8,2,9216]{2,1,0:T(2,128)(2,1)} reshape(bf16[192,16,48]{2,1,0:T(8,128)(2,1)S(1)} %bitcast.81) | data formatting | bytes 589824
  75.2 3.4 %all-to-all-start.5 = ((bf16[8,2,9216]{2,1,0:T(2,128)(2,1)}), bf16[8,2,9216]{2,1,0:T(2,128)(2,1)S(1)}, u32[]{:S(2)}, u32[]{:S(2)}) async-start(bf16[8,2,9216]{2,1,0:T(2,128)(2,1)} %reshape.64), calls=%async_computation.5 | async-start | bytes 589824 | tf_op jit(solution)/shard_map/all_to_all | solution.py:61
  79.3 0.5 fusion.10
  79.9 5.1 %all-to-all-done.5 = bf16[8,2,9216]{2,1,0:T(2,128)(2,1)S(1)} async-done(((bf16[8,2,9216]{2,1,0:T(2,128)(2,1)}), bf16[8,2,9216]{2,1,0:T(2,128)(2,1)S(1)}, u32[]{:S(2)}, u32[]{:S(2)}) %all-to-all-start.5) | async-done | bytes 294944 | tf_op jit(solution)/shard_map/all_to_all | solution.py:61
  85.0 0.8 reshape.65
  86.3 0.4 fusion.7
  87.2 1.0 %fusion.11 = bf16[48,24,128]{2,1,0:T(8,128)(2,1)} fusion(f32[48,24,128]{2,1,0:T(8,128)S(1)} %fusion.10, bf16[48,24,128]{2,1,0:T(8,128)(2,1)S(1)} %copy.103, bf16[128,128,1]{1,0,2:T(8,128)(2,1)S(1)} %bitcast.91), kind=kOutput, calls=%fused_computation.15 | convolution fusion | flops 38043648 | bytes 1212416 | tf_op jit(solution)/shard_map/xyc,cd->xyd/dot_general | solution.py:76
  (42 shorter events, 2.9 us)
Async XLA Ops:
  0.0 2.9 %copy-start = (bf16[128,512]{1,0:T(8,128)(2,1)S(1)}, bf16[128,512]{1,0:T(8,128)(2,1)}, u32[]{:S(2)}) copy-start(bf16[128,512]{1,0:T(8,128)(2,1)} %param.11) | copy-start | bytes 393220
  8.2 16.0 %all-to-all-start = ((bf16[4,2,18432]{2,1,0:T(2,128)(2,1)}), bf16[4,2,18432]{2,1,0:T(2,128)(2,1)S(1)}, u32[]{:S(2)}, u32[]{:S(2)}) async-start(bf16[4,2,18432]{2,1,0:T(2,128)(2,1)} %reshape.60), calls=%async_computation | async-start | bytes 589824 | tf_op jit(solution)/shard_map/all_to_all | solution.py:9
  24.2 11.6 %all-to-all-start.2 = ((bf16[4,2,18432]{2,1,0:T(2,128)(2,1)}), bf16[4,2,18432]{2,1,0:T(2,128)(2,1)S(1)}, u32[]{:S(2)}, u32[]{:S(2)}) async-start(bf16[4,2,18432]{2,1,0:T(2,128)(2,1)} %reshape.62), calls=%async_computation.2 | async-start | bytes 589824 | tf_op jit(solution)/shard_map/all_to_all | solution.py:46
  35.8 11.2 %all-to-all-start.1 = ((bf16[192,24,32]{0,1,2:T(8,128)(2,1)}), bf16[192,24,32]{0,1,2:T(8,128)(2,1)S(1)}, u32[]{:S(2)}, u32[]{:S(2)}) async-start(bf16[192,24,32]{0,1,2:T(8,128)(2,1)} %reshape.50), calls=%async_computation.1 | async-start | bytes 786432 | tf_op jit(solution)/shard_map/all_to_all | solution.py:52
  47.0 10.8 %all-to-all-start.3 = ((bf16[192,24,32]{0,1,2:T(8,128)(2,1)}), bf16[192,24,32]{0,1,2:T(8,128)(2,1)S(1)}, u32[]{:S(2)}, u32[]{:S(2)}) async-start(bf16[192,24,32]{0,1,2:T(8,128)(2,1)} %reshape.59), calls=%async_computation.3 | async-start | bytes 786432 | tf_op jit(solution)/shard_map/all_to_all | solution.py:45
  72.6 6.1 %copy-start.5 = (f32[128]{0:T(128)S(1)}, f32[128]{0:T(128)}, u32[]{:S(2)}) copy-start(f32[128]{0:T(128)} %param.14) | copy-start | bytes 1540
  72.6 6.3 %copy-start.6 = (f32[128]{0:T(128)S(1)}, f32[128]{0:T(128)}, u32[]{:S(2)}) copy-start(f32[128]{0:T(128)} %param.13) | copy-start | bytes 1540
  72.6 6.6 %copy-start.2 = (bf16[128,128]{1,0:T(8,128)(2,1)S(1)}, bf16[128,128]{1,0:T(8,128)(2,1)}, u32[]{:S(2)}) copy-start(bf16[128,128]{1,0:T(8,128)(2,1)} %param.15) | copy-start | bytes 98308
  72.6 6.6 %copy-start.1 = (bf16[48,24,128]{2,1,0:T(8,128)(2,1)S(1)}, bf16[48,24,128]{2,1,0:T(8,128)(2,1)}, u32[]{:S(2)}) copy-start(bf16[48,24,128]{2,1,0:T(8,128)(2,1)} %param.8) | copy-start | bytes 884740
  72.6 6.6 %copy-start.3 = (f32[128]{0:T(128)S(1)}, f32[128]{0:T(128)}, u32[]{:S(2)}) copy-start(f32[128]{0:T(128)} %param.10) | copy-start | bytes 1540
  72.7 6.6 %copy-start.4 = (f32[128]{0:T(128)S(1)}, f32[128]{0:T(128)}, u32[]{:S(2)}) copy-start(f32[128]{0:T(128)} %param.9) | copy-start | bytes 1540
  72.7 6.6 %copy-start.7 = (bf16[128,128]{1,0:T(8,128)(2,1)S(1)}, bf16[128,128]{1,0:T(8,128)(2,1)}, u32[]{:S(2)}) copy-start(bf16[128,128]{1,0:T(8,128)(2,1)} %param.12) | copy-start | bytes 98308
  75.2 9.7 %all-to-all-start.5 = ((bf16[8,2,9216]{2,1,0:T(2,128)(2,1)}), bf16[8,2,9216]{2,1,0:T(2,128)(2,1)S(1)}, u32[]{:S(2)}, u32[]{:S(2)}) async-start(bf16[8,2,9216]{2,1,0:T(2,128)(2,1)} %reshape.64), calls=%async_computation.5 | async-start | bytes 589824 | tf_op jit(solution)/shard_map/all_to_all | solution.py:61
